TPU v7x, 32 devices: a whole 2x2x4 slice. The times are simulated.
32 devices in a mesh: seq: 8 (over y, x, core), tp: 4 (over z).
Axes of the slice: x: 2, y: 2, z: 4, core: 2. Of those that a mesh axis runs over, the one named last changes fastest.
Arguments:
- queries: bfloat16 [4096, 8192], P('seq', 'tp'), may hold values from -6 to 6
- keys: bfloat16 [4096, 8192], P('seq', 'tp'), may hold values from -0.5 to 0.5
- values: bfloat16 [4096, 8192], P('seq', 'tp'), may hold values from -6 to 6
- gate: bfloat16 [4096, 8192], P('seq', 'tp'), may hold values from -6 to 6
- log_decay: float32 [4096, 64], P('seq', 'tp'), may hold values from -0.8 to 0
- out_grad: bfloat16 [4096, 8192], P('seq', 'tp'), may hold values from -6 to 6
Outputs:
- output: bfloat16 [4096, 8192], P('seq', 'tp')
- query_grad: bfloat16 [4096, 8192], P('seq', 'tp')
- key_grad: bfloat16 [4096, 8192], P('seq', 'tp')
- value_grad: bfloat16 [4096, 8192], P('seq', 'tp')
- gate_grad: bfloat16 [4096, 8192], P('seq', 'tp')
All inputs are finite; a program needn't handle non-finite values.
Results may differ from a plain program's by a relative error of at most 0.0051.
Values sent between devices are 32-bit elements; how exact they have to be, the bound alone decides.
A program may use at most 128 MiB of HBM per device.

v0:
```python
import jax
import jax.numpy as jnp
from jax import lax
from jax.sharding import PartitionSpec as P

HEAD_COUNT = 64
HEAD = 128


HIGH = lax.Precision.HIGHEST


def decay_table(within):
    gap = within.T[:, :, None] - within.T[:, None, :]
    rows = lax.broadcasted_iota(jnp.int32, gap.shape, 1)
    cols = lax.broadcasted_iota(jnp.int32, gap.shape, 2)
    return jnp.where(rows >= cols, jnp.exp(jnp.minimum(gap, 0.0)), 0.0)


def shards(queries, keys, values, gate, log_decay, out_grad):
    tokens = queries.shape[0]
    heads = log_decay.shape[1]
    width = HEAD_COUNT * HEAD
    qh = queries.reshape(tokens, heads, HEAD)
    kh = keys.reshape(tokens, heads, HEAD)
    vh = values.reshape(tokens, heads, HEAD)
    within = jnp.cumsum(log_decay, axis=0)
    last = within[-1]
    decay = decay_table(within)
    scores = jnp.einsum("thd,shd->hts", qh, kh, preferred_element_type=jnp.float32)
    probs = (scores * decay).astype(jnp.bfloat16)
    intra = jnp.einsum("hts,shd->thd", probs, vh, preferred_element_type=jnp.float32)
    qf = qh.astype(jnp.float32)
    kf = kh.astype(jnp.float32)
    vf = vh.astype(jnp.float32)
    grow = jnp.exp(within)[:, :, None]
    tail = jnp.exp(last[None, :] - within)[:, :, None]
    local = jnp.einsum("thd,the->hde", kf * tail, vf, precision=HIGH)
    rates_all = lax.all_gather(last[None, :], "seq", axis=0, tiled=True)
    summed = jnp.cumsum(rates_all, axis=0)
    previous = summed - rates_all
    mine = lax.axis_index("seq")
    before = lax.dynamic_slice_in_dim(previous, mine, 1, 0)[0]
    mine_sum = lax.dynamic_slice_in_dim(summed, mine, 1, 0)[0]
    piece = lax.all_gather(local[None], "seq", axis=0, tiled=True)
    count = piece.shape[0]
    position = jnp.arange(count, dtype=jnp.int32)
    rows = summed
    weights = jnp.where(
        (position < mine)[:, None], jnp.exp(jnp.minimum(before[None, :] - rows, 0.0)), 0.0
    )
    state = jnp.einsum("mh,mhde->hde", weights, piece, precision=HIGH)
    inter = grow * jnp.einsum("thd,hde->the", qf, state, precision=HIGH)
    attn = (intra + inter).reshape(tokens, heads * HEAD)
    squares = lax.psum(jnp.sum(attn * attn, axis=1), "tp")
    scale = lax.rsqrt(squares / width + 1e-06)
    normed = attn * scale[:, None]
    sig = jax.nn.sigmoid(gate.astype(jnp.float32))
    output = (normed * sig).astype(jnp.bfloat16)
    upstream = out_grad.astype(jnp.float32)
    dnorm = upstream * sig
    gate_grad = (upstream * normed * sig * (1.0 - sig)).astype(jnp.bfloat16)
    center = lax.psum(jnp.sum(dnorm * normed, axis=1), "tp") / width
    attn_grad = (scale[:, None] * (dnorm - normed * center[:, None])).astype(jnp.bfloat16)
    grad_h = attn_grad.reshape(tokens, heads, HEAD)
    gradf = grad_h.astype(jnp.float32)
    weighted = jnp.einsum("thd,the->hde", qf * grow, gradf, precision=HIGH)
    piece = lax.all_gather(weighted[None], "seq", axis=0, tiled=True)
    count = piece.shape[0]
    position = jnp.arange(count, dtype=jnp.int32)
    rows = previous
    weights = jnp.where(
        (position > mine)[:, None], jnp.exp(jnp.minimum(rows - mine_sum[None, :], 0.0)), 0.0
    )
    grad_state = jnp.einsum("mh,mhde->hde", weights, piece, precision=HIGH)
    pgrad = (
        jnp.einsum("thd,shd->hts", grad_h, vh, preferred_element_type=jnp.float32) * decay
    ).astype(jnp.bfloat16)
    query_grad = jnp.einsum(
        "hts,shd->thd", pgrad, kh, preferred_element_type=jnp.float32
    ) + grow * jnp.einsum("the,hde->thd", gradf, state, precision=HIGH)
    key_grad = jnp.einsum(
        "hts,thd->shd", pgrad, qh, preferred_element_type=jnp.float32
    ) + tail * jnp.einsum("the,hde->thd", vf, grad_state, precision=HIGH)
    value_grad = jnp.einsum(
        "hts,thd->shd", probs, grad_h, preferred_element_type=jnp.float32
    ) + tail * jnp.einsum("thd,hde->the", kf, grad_state, precision=HIGH)
    flat = heads * HEAD
    return (
        output,
        query_grad.reshape(tokens, flat).astype(jnp.bfloat16),
        key_grad.reshape(tokens, flat).astype(jnp.bfloat16),
        value_grad.reshape(tokens, flat).astype(jnp.bfloat16),
        gate_grad,
    )


def solution(mesh):
    in_specs = (
        P("seq", "tp"),
        P("seq", "tp"),
        P("seq", "tp"),
        P("seq", "tp"),
        P("seq", "tp"),
        P("seq", "tp"),
    )
    out_specs = (P("seq", "tp"), P("seq", "tp"), P("seq", "tp"), P("seq", "tp"), P("seq", "tp"))
    return jax.shard_map(shards, mesh=mesh, in_specs=in_specs, out_specs=out_specs, check_vma=False)
```

profile of v0, /device:TPU:1, one launch (start us, length us, event | category | flops | bytes accessed | tf_op | source)
XLA Modules:
  0.0 225.1 jit_solution(16245375987942641645)
XLA Ops:
  7.2 0.9 copy_bitcast_fusion.1
  8.1 1.1 reduce-window.6
  9.8 3.9 %copy.81 = bf16[512,2048]{0,1:T(8,128)(2,1)} copy(bf16[512,2048]{1,0:T(8,128)(2,1)} %param.7) | data formatting | bytes 4194304 | tf_op args[1]
  13.8 5.0 %fusion.15 = f32[16,128,128]{2,1,0:T(8,128)} fusion(bf16[512,16,128]{0,2,1:T(8,128)(2,1)} %bitcast.124, f32[512,16]{0,1:T(8,128)S(1)} %get-tuple-element.31, bf16[512,2048]{1,0:T(8,128)(2,1)S(1)} %copy-done), kind=kOutput, calls=%fused_computation.31 | convolution fusion | flops 1612709888 | bytes 5275648 | tf_op jit(solution)/shard_map/thd,the->hde/dot_general | solution.py:38
  18.8 10.3 %all-gather.2 = f32[8,1,16]{2,1,0:T(1,128)S(1)} all-gather(f32[1,1,16]{2,1,0:T(1,128)S(1)} %bitcast.138), channel_id=1, replica_groups=mesh['seq'=8,'tp'=4] {'seq'}, dimensions={0}, use_global_device_ids=true | all-gather | bytes 576 | tf_op jit(solution)/shard_map/all_gather | solution.py:39
  29.4 4.0 %copy.80 = bf16[512,2048]{0,1:T(8,128)(2,1)} copy(bf16[512,2048]{1,0:T(8,128)(2,1)} %param.6) | data formatting | bytes 4194304 | tf_op args[0]
  33.4 7.3 %multiply_convert_fusion.1 = bf16[16,512,512]{2,1,0:T(8,128)(2,1)S(1)} fusion(bf16[512,16,128]{0,2,1:T(8,128)(2,1)} %bitcast.116, bf16[512,16,128]{0,2,1:T(8,128)(2,1)} %bitcast.125, f32[16,512]{1,0:T(8,128)S(1)} %get-tuple-element.33), kind=kOutput, calls=%fused_computation.1 | convolution fusion | flops 1098907648 | bytes 12615680 | tf_op jit(solution)/shard_map/thd,shd->hts/dot_general | solution.py:30
  40.7 3.2 %copy-done.1 = bf16[16,512,512]{2,1,0:T(8,128)(2,1)} copy-done((bf16[16,512,512]{2,1,0:T(8,128)(2,1)}, bf16[16,512,512]{2,1,0:T(8,128)(2,1)S(1)}, u32[]{:S(2)}) %copy-start.1) | copy-done | bytes 8388632
  43.9 4.8 %fusion.18 = f32[16,512,128]{1,2,0:T(8,128)} fusion(bf16[16,512,512]{2,1,0:T(8,128)(2,1)S(1)} %multiply_convert_fusion.1, bf16[512,2048]{1,0:T(8,128)(2,1)S(1)} %copy-done), kind=kOutput, calls=%fused_computation.34 | convolution fusion | flops 1073741824 | bytes 14680064 | tf_op jit(solution)/shard_map/hts,shd->thd/dot_general | solution.py:32
  48.7 27.0 %all-gather.6.cloned.1.call-done = f32[128,128,128]{2,1,0:T(8,128)} async-done(((f32[16,128,128]{2,1,0:T(8,128)}), f32[128,128,128]{2,1,0:T(8,128)}) %all-gather.6.cloned.1.call-update) | async-done | bytes 8388624 | tf_op jit(solution)/shard_map/all_gather | solution.py:45
  75.7 15.7 %fusion = f32[16,1,128,128]{3,1,2,0:T(1,128)S(1)} fusion(f32[8,16,1,1]{0,2,3,1:T(1,128)S(1)} %copy.104, f32[8,16,128,128]{3,2,1,0:T(8,128)} %bitcast.131), kind=kOutput, calls=%fused_computation.5 | convolution fusion | flops 25165824 | bytes 9437696 | tf_op jit(solution)/shard_map/mh,mhde->hde/dot_general | solution.py:52
  91.4 4.3 %multiply_reduce_fusion.2 = (f32[512]{0:T(512)S(1)}, f32[512,16,128]{0,2,1:T(8,128)}) fusion(f32[16,128,128]{2,1,0:T(8,128)S(1)} %bitcast.129, bf16[512,16,128]{0,2,1:T(8,128)(2,1)S(1)} %bitcast.118, f32[512,16]{0,1:T(8,128)S(1)} %get-tuple-element.30, f32[16,512,128]{1,2,0:T(8,128)S(1)} %copy-done.10), kind=kOutput, calls=%fused_computation.30 | convolution fusion | flops 1614806528 | bytes 11569152 | tf_op jit(solution)/shard_map/thd,hde->the/dot_general | solution.py:53
  95.6 5.4 %copy.90 = f32[512,2048]{1,0:T(8,128)} copy(f32[512,2048]{0,1:T(8,128)} %bitcast.128) | data formatting | bytes 8388608 | tf_op jit(solution)/shard_map/reshape | solution.py:54
  101.0 9.6 %psum.14 = f32[512]{0:T(512)S(1)} all-reduce(f32[512]{0:T(512)S(1)} %get-tuple-element.34), channel_id=1, replica_groups=mesh['seq'=8,'tp'=4] {'tp'}, use_global_device_ids=true, to_apply=%region_4.5 | all-reduce | flops 512 | bytes 4096 | tf_op jit(solution)/shard_map/psum | solution.py:55
  110.6 4.9 %multiply_reduce_fusion.1 = f32[512]{0:T(512)S(1)} fusion(f32[512,2048]{1,0:T(8,128)} %copy.90, bf16[512,2048]{1,0:T(8,128)(2,1)} %param.11, f32[512]{0:T(512)S(1)} %add_rsqrt_fusion, bf16[512,2048]{1,0:T(8,128)(2,1)} %param.9), kind=kLoop, calls=%fused_computation.27 | loop fusion | flops 9436672 | bytes 8392704 | tf_op jit(solution)/shard_map/reduce_sum | solution.py:63
  115.5 6.6 %psum.15 = f32[512]{0:T(512)S(1)} all-reduce(f32[512]{0:T(512)S(1)} %multiply_reduce_fusion.1), channel_id=1, replica_groups=mesh['seq'=8,'tp'=4] {'tp'}, use_global_device_ids=true, to_apply=%region_6.7 | all-reduce | flops 512 | bytes 4096 | tf_op jit(solution)/shard_map/psum | solution.py:63
  122.2 7.1 %fusion.4 = (bf16[512,2048]{1,0:T(8,128)(2,1)}, bf16[512,2048]{1,0:T(8,128)(2,1)}, bf16[512,2048]{1,0:T(8,128)(2,1)}) fusion(bf16[512,2048]{1,0:T(8,128)(2,1)} %param.11, f32[512,2048]{1,0:T(8,128)} %copy.90, f32[512]{0:T(512)S(1)} %add_rsqrt_fusion, bf16[512,2048]{1,0:T(8,128)(2,1)} %param.9, f32[512]{0:T(512)S(1)} %broadcast_multiply_fusion), kind=kLoop, calls=%fused_computation.11 | loop fusion | flops 18874368 | bytes 14684160 | tf_op jit(solution)/shard_map/convert_element_type | solution.py:62
  129.3 3.9 %copy.118 = bf16[512,2048]{0,1:T(8,128)(2,1)} copy(bf16[512,2048]{1,0:T(8,128)(2,1)} %get-tuple-element.28) | data formatting | bytes 4194304 | tf_op jit(solution)/shard_map/reshape | solution.py:65
  133.2 5.4 %fusion.12 = f32[16,128,128]{2,1,0:T(8,128)} fusion(bf16[512,16,128]{0,2,1:T(8,128)(2,1)} %bitcast.120, bf16[512,16,128]{0,2,1:T(8,128)(2,1)} %bitcast.117, f32[512,16]{0,1:T(8,128)S(1)} %get-tuple-element.30), kind=kOutput, calls=%fused_computation.23 | convolution fusion | flops 1612709888 | bytes 5275648 | tf_op jit(solution)/shard_map/thd,the->hde/dot_general | solution.py:67
  138.6 5.4 %multiply_convert_fusion = bf16[16,512,512]{2,1,0:T(8,128)(2,1)S(1)} fusion(bf16[512,16,128]{0,2,1:T(8,128)(2,1)} %bitcast.121, f32[16,512]{1,0:T(8,128)S(1)} %get-tuple-element.33, bf16[512,2048]{1,0:T(8,128)(2,1)S(1)} %copy-done), kind=kOutput, calls=%fused_computation | convolution fusion | flops 1098907648 | bytes 12615680 | tf_op jit(solution)/shard_map/thd,shd->hts/dot_general | solution.py:77
  144.0 4.8 %fusion.30 = f32[16,512,128]{1,2,0:T(8,128)} fusion(bf16[16,512,512]{2,1,0:T(8,128)(2,1)S(1)} %multiply_convert_fusion, bf16[512,16,128]{0,2,1:T(8,128)(2,1)S(1)} %bitcast.126), kind=kOutput, calls=%fused_computation.61 | convolution fusion | flops 1073741824 | bytes 14680064 | tf_op jit(solution)/shard_map/hts,shd->thd/dot_general | solution.py:79
  149.5 6.0 %fusion.10 = bf16[512,16,128]{0,2,1:T(8,128)(2,1)} fusion(f32[16,512,128]{1,2,0:T(8,128)} %fusion.30, f32[16,128,128]{2,1,0:T(8,128)S(1)} %bitcast.130, bf16[512,16,128]{0,2,1:T(8,128)(2,1)S(1)} %bitcast.123, f32[512,16]{0,1:T(8,128)S(1)} %get-tuple-element.30), kind=kOutput, calls=%fused_computation.20 | convolution fusion | flops 1613758464 | bytes 9469952 | tf_op jit(solution)/shard_map/the,hde->thd/dot_general | solution.py:81
  155.6 4.1 %copy.99 = bf16[512,2048]{1,0:T(8,128)(2,1)} copy(bf16[512,2048]{0,1:T(8,128)(2,1)} %bitcast.133) | data formatting | bytes 4194304
  159.7 7.5 %fusion.31 = f32[16,128,512]{2,1,0:T(8,128)} fusion(bf16[512,16,128]{0,2,1:T(8,128)(2,1)} %bitcast.122, bf16[16,512,512]{2,1,0:T(8,128)(2,1)} %copy-done.1), kind=kOutput, calls=%fused_computation.62 | convolution fusion | flops 1073741824 | bytes 14680064 | tf_op jit(solution)/shard_map/hts,thd->shd/dot_general | solution.py:85
  167.2 0.8 copy-done.5
  168.0 3.2 %fusion.32 = f32[16,512,128]{1,2,0:T(8,128)} fusion(bf16[512,16,128]{0,2,1:T(8,128)(2,1)S(1)} %bitcast.119, bf16[16,512,512]{2,1,0:T(8,128)(2,1)S(1)} %copy-done.3), kind=kOutput, calls=%fused_computation.63 | convolution fusion | flops 1073741824 | bytes 14680064 | tf_op jit(solution)/shard_map/hts,thd->shd/dot_general | solution.py:82
  171.2 24.2 %all-gather.8.cloned.1.call-done = f32[128,128,128]{2,1,0:T(8,128)} async-done(((f32[16,128,128]{2,1,0:T(8,128)}), f32[128,128,128]{2,1,0:T(8,128)}) %all-gather.8.cloned.1.call-update) | async-done | bytes 8388624 | tf_op jit(solution)/shard_map/all_gather | solution.py:68
  195.5 4.3 %multiply_reduce_fusion = f32[16,128,128]{2,1,0:T(8,128)S(1)} fusion(f32[16,8,128,128]{3,2,0,1:T(8,128)} %bitcast.132, f32[16,8]{0,1:T(8,128)S(1)} %get-tuple-element.25), kind=kLoop, calls=%fused_computation.4 | loop fusion | flops 3932160 | bytes 9437696 | tf_op jit(solution)/shard_map/mh,mhde->hde/dot_general | solution.py:75
  200.7 3.7 %fusion.6 = bf16[512,16,128]{0,2,1:T(8,128)(2,1)} fusion(f32[16,128,512]{2,1,0:T(8,128)S(1)} %copy-done.7, f32[16,128,128]{2,1,0:T(8,128)S(1)} %multiply_reduce_fusion, bf16[512,16,128]{0,2,1:T(8,128)(2,1)S(1)} %bitcast.127, f32[512,16]{0,1:T(8,128)S(1)} %get-tuple-element.31), kind=kOutput, calls=%fused_computation.14 | convolution fusion | flops 1613758464 | bytes 9469952 | tf_op jit(solution)/shard_map/thd,hde->the/dot_general | solution.py:87
  204.4 3.9 %copy.101 = bf16[512,2048]{1,0:T(8,128)(2,1)} copy(bf16[512,2048]{0,1:T(8,128)(2,1)} %bitcast.135) | data formatting | bytes 4194304
  208.3 5.6 %fusion.8 = bf16[512,16,128]{0,2,1:T(8,128)(2,1)} fusion(f32[16,512,128]{1,2,0:T(8,128)} %fusion.32, f32[16,128,128]{2,1,0:T(8,128)S(1)} %multiply_reduce_fusion, f32[512,16]{0,1:T(8,128)S(1)} %get-tuple-element.31, bf16[512,2048]{1,0:T(8,128)(2,1)S(1)} %copy-done), kind=kOutput, calls=%fused_computation.17 | convolution fusion | flops 1613758464 | bytes 9469952 | tf_op jit(solution)/shard_map/the,hde->thd/dot_general | solution.py:84
  213.9 3.9 %copy.100 = bf16[512,2048]{1,0:T(8,128)(2,1)} copy(bf16[512,2048]{0,1:T(8,128)(2,1)} %bitcast.134) | data formatting | bytes 4194304
  (39 shorter events, 2.7 us)
Async XLA Ops:
  7.2 6.6 %copy-start = (bf16[512,2048]{1,0:T(8,128)(2,1)S(1)}, bf16[512,2048]{1,0:T(8,128)(2,1)}, u32[]{:S(2)}) copy-start(bf16[512,2048]{1,0:T(8,128)(2,1)} %param.8) | copy-start | bytes 6291460
  7.2 68.5 %all-gather.6.cloned.1.call-start = ((), (), s32[]{:S(2)}) async-start(), calls=%async_computation | async-start | bytes 9437184 | tf_op jit(solution)/shard_map/all_gather | solution.py:45
  18.8 176.7 %all-gather.8.cloned.1.call-start = ((), (), s32[]{:S(2)}) async-start(), calls=%async_computation.1 | async-start | bytes 9437184 | tf_op jit(solution)/shard_map/all_gather | solution.py:68
  40.7 3.2 %copy-start.1 = (bf16[16,512,512]{2,1,0:T(8,128)(2,1)}, bf16[16,512,512]{2,1,0:T(8,128)(2,1)S(1)}, u32[]{:S(2)}) copy-start(bf16[16,512,512]{2,1,0:T(8,128)(2,1)S(1)} %multiply_convert_fusion.1) | copy-start | bytes 25165828
  75.7 15.7 %copy-start.4 = (bf16[512,2048]{0,1:T(8,128)(2,1)S(1)}, bf16[512,2048]{0,1:T(8,128)(2,1)}, u32[]{:S(2)}) copy-start(bf16[512,2048]{0,1:T(8,128)(2,1)} %copy.80) | copy-start | bytes 6291460
  75.7 15.7 %copy-start.10 = (f32[16,512,128]{1,2,0:T(8,128)S(1)}, f32[16,512,128]{1,2,0:T(8,128)}, u32[]{:S(2)}) copy-start(f32[16,512,128]{1,2,0:T(8,128)} %fusion.18) | copy-start | bytes 12582916
  138.6 5.4 %copy-start.8 = (bf16[512,2048]{0,1:T(8,128)(2,1)S(1)}, bf16[512,2048]{0,1:T(8,128)(2,1)}, u32[]{:S(2)}) copy-start(bf16[512,2048]{0,1:T(8,128)(2,1)} %copy.81) | copy-start | bytes 6291460
  144.0 5.6 %copy-start.2 = (bf16[16,512,512]{2,1,0:T(8,128)(2,1)}, bf16[16,512,512]{2,1,0:T(8,128)(2,1)S(1)}, u32[]{:S(2)}) copy-start(bf16[16,512,512]{2,1,0:T(8,128)(2,1)S(1)} %multiply_convert_fusion) | copy-start | bytes 25165828
  144.0 5.5 %copy-start.6 = (bf16[512,2048]{0,1:T(8,128)(2,1)S(1)}, bf16[512,2048]{0,1:T(8,128)(2,1)}, u32[]{:S(2)}) copy-start(bf16[512,2048]{0,1:T(8,128)(2,1)} %copy.118) | copy-start | bytes 6291460
  159.7 7.5 %copy-start.3 = (bf16[16,512,512]{2,1,0:T(8,128)(2,1)S(1)}, bf16[16,512,512]{2,1,0:T(8,128)(2,1)}, u32[]{:S(2)}) copy-start(bf16[16,512,512]{2,1,0:T(8,128)(2,1)} %copy-done.2) | copy-start | bytes 25165828
  159.7 8.3 %copy-start.5 = (bf16[512,2048]{0,1:T(8,128)(2,1)S(1)}, bf16[512,2048]{0,1:T(8,128)(2,1)}, u32[]{:S(2)}) copy-start(bf16[512,2048]{0,1:T(8,128)(2,1)} %copy.80) | copy-start | bytes 6291460
  195.5 4.6 %copy-start.7 = (f32[16,128,512]{2,1,0:T(8,128)S(1)}, f32[16,128,512]{2,1,0:T(8,128)}, u32[]{:S(2)}) copy-start(f32[16,128,512]{2,1,0:T(8,128)} %fusion.31) | copy-start | bytes 12582916
  195.5 5.3 %copy-start.9 = (bf16[512,2048]{0,1:T(8,128)(2,1)S(1)}, bf16[512,2048]{0,1:T(8,128)(2,1)}, u32[]{:S(2)}) copy-start(bf16[512,2048]{0,1:T(8,128)(2,1)} %copy.81) | copy-start | bytes 6291460
Sparse Core Ops, SparseCore 0:
  18.9 56.7 all-gather.5
  138.7 56.6 all-gather.7
where the time goes:
time: 229 us; the launch traced here: 225 us
  matrix products  78.5 us (34%)
  waiting for transfers between devices  51.3 us (22%)
  local copies, waits for them, and re-layouts  36.3 us (16%)
  blocking collectives  26.6 us (12%)
  other arithmetic  17.8 us (8%)
  between operations  14.6 us (6%)
    all_gather x1, waiting for transfers between devices, shards(): piece = lax.all_gather(local[None], 'seq', axis=0, tiled=True)  27 us
    unnamed x27, local copies, waits for them, and re-layouts  25.7 us
    all_gather x1, waiting for transfers between devices, shards(): piece = lax.all_gather(weighted[None], 'seq', axis=0, tiled=True)  24.2 us
    dot_general x1, matrix products, shards(): state = jnp.einsum('mh,mhde->hde', weights, piece, precision=HIGH)  15.7 us
    all_gather x1, blocking collectives, shards(): rates_all = lax.all_gather(last[None, :], 'seq', axis=0, tiled=True)  10.3 us
    psum x1, blocking collectives, shards(): squares = lax.psum(jnp.sum(attn * attn, axis=1), 'tp')  9.63 us
    dot_general x1, matrix products, shards(): jnp.einsum('hts,thd->shd', probs, grad_h, preferred_element_type=jnp.floa...  7.48 us
    dot_general x1, matrix products, shards(): jnp.einsum('thd,shd->hts', qh, kh, preferred_element_type=jnp.float32)  7.31 us
  transfers between devices with their start and end apart: 2, of which 2 were waited for; matrix products, arithmetic and copies ran while one was open for 21% of the time, Pallas kernels for 0%

commit v1 on v0

v1 whole, which is shorter than its diff:
```python
import functools

import jax
import jax.numpy as jnp
from jax import lax
from jax.experimental import pallas as pl
from jax.experimental.pallas import tpu as pltpu
from jax.sharding import PartitionSpec as P

MESH = pl.DeviceIdType.MESH
F32 = jnp.float32
BF16 = jnp.bfloat16
HIGH = lax.Precision.HIGHEST
EXTRA = 8
CHUNKS = 4


def nt(a, b):
    return lax.dot_general(a, b, (((1,), (1,)), ((), ())), preferred_element_type=F32)


def tn(a, b):
    return lax.dot_general(a, b, (((0,), (0,)), ((), ())), preferred_element_type=F32)


def nn(a, b):
    return lax.dot_general(a, b, (((1,), (0,)), ((), ())), preferred_element_type=F32)


def kernel(
    n_seq, n_tp, heads, dim, tokens,
    q_hbm, k_hbm, v_hbm, gate_hbm, rate_hbm, up_hbm,
    out_hbm, dq_hbm, dk_hbm, dv_hbm, gg_hbm,
    q, k, v, gate, rate, up, rates_wide, rows, cols, attn, dvp, grad, probs,
    own, other, sent, got, edge, far, state, sums, sums_in, scale_ref, center_ref,
    in_sem, out_sem, s0_send, s0_recv, st_send, st_recv, fin_send, fin_recv, tp_send, tp_recv,
):
    width = heads * dim * n_tp
    half = heads // 2
    bits = n_seq.bit_length() - 1
    chips = bits - 1
    per = half // CHUNKS
    block = min(256, tokens)
    nb = tokens // block
    me = lax.axis_index("seq")
    z = lax.axis_index("tp")
    core = lax.rem(me, 2)

    def bit_of(b):
        return lax.rem(me // (1 << b), 2)

    def partner(b):
        return (me + (1 << b) * (1 - 2 * bit_of(b)), z)

    def take(d, b):
        bit = bit_of(b).astype(F32)
        return bit if d == 0 else 1.0 - bit

    loads = []
    for i, (a, b) in enumerate(
        ((rate_hbm, rate), (k_hbm, k), (v_hbm, v), (q_hbm, q), (up_hbm, up), (gate_hbm, gate))
    ):
        c = pltpu.make_async_copy(a, b, in_sem.at[i])
        c.start()
        loads.append(c)

    barrier = pltpu.get_barrier_semaphore()
    for b in range(bits):
        pl.semaphore_signal(barrier, inc=1, device_id=partner(b), device_id_type=MESH)
    for d in range(1, n_tp):
        pl.semaphore_signal(
            barrier, inc=1, device_id=(me, lax.rem(z + d, n_tp)), device_id_type=MESH
        )

    def lane(h):
        return pl.ds(pl.multiple_of(h * dim, dim), dim)

    def pairs(body):
        @pl.loop(0, heads // 2)
        def _(i):
            body(2 * i)
            body(2 * i + 1)

    loads[0].wait()
    rates_wide[...] = jnp.zeros_like(rates_wide)
    rates_wide[:, 0:heads] = rate[...]
    tri = (
        lax.broadcasted_iota(jnp.int32, (tokens, tokens), 0)
        >= lax.broadcasted_iota(jnp.int32, (tokens, tokens), 1)
    ).astype(F32)
    within = lax.dot_general(
        tri, rates_wide[...], (((1,), (0,)), ((), ())), precision=HIGH, preferred_element_type=F32
    )
    rows[...] = within.T
    for h in range(heads):
        cols[h] = jnp.broadcast_to(within[:, h : h + 1], (tokens, dim))

    loads[1].wait()
    loads[2].wait()

    def make_local(h):
        last = cols[h, tokens - 1 : tokens, :]
        scaled = (k[:, lane(h)].astype(F32) * jnp.exp(last - cols[h])).astype(BF16)
        own[0, h, 0:dim, :] = tn(scaled, v[:, lane(h)])
        own[0, h, dim : dim + EXTRA, :] = jnp.broadcast_to(last, (EXTRA, dim))

    pairs(make_local)

    def s0_copy(d):
        return pltpu.make_async_remote_copy(
            src_ref=own.at[d], dst_ref=other.at[d], send_sem=s0_send.at[d],
            recv_sem=s0_recv.at[d], device_id=partner(0), device_id_type=MESH,
        )

    def st_copy(d, s, c):
        part = pl.ds(c * per, per)
        return pltpu.make_async_remote_copy(
            src_ref=sent.at[d, s, part], dst_ref=got.at[d, s, part], send_sem=st_send.at[d, s, c],
            recv_sem=st_recv.at[d, s, c], device_id=partner(s + 1), device_id_type=MESH,
        )

    def fin_copy(d, c):
        part = pl.ds(c * per, per)
        return pltpu.make_async_remote_copy(
            src_ref=edge.at[d, part], dst_ref=far.at[d, part], send_sem=fin_send.at[d, c],
            recv_sem=fin_recv.at[d, c], device_id=partner(0), device_id_type=MESH,
        )

    def joined(f, mine, theirs):
        dm, dt = mine[dim : dim + 1], theirs[dim : dim + 1]
        total = jnp.exp(dt * (1.0 - f)) * mine[0:dim] + jnp.exp(dm * f) * theirs[0:dim]
        return total, mine[dim:] + theirs[dim:]

    def step_first(d):
        s0_copy(d).wait_recv()
        f = take(d, 0)
        for c in range(CHUNKS):

            @pl.loop(0, per)
            def _(i):
                hh = c * per + i
                h = core * half + hh
                total, span = joined(f, own[d, h], other[d, h])
                sent[d, 0, hh, 0:dim, :] = total
                sent[d, 0, hh, dim:, :] = span
                edge[d, hh] = jnp.zeros((dim + EXTRA, dim), F32)

            if chips:
                st_copy(d, 0, c).start()
            else:
                fin_copy(d, c).start()

    def step(d, s, c):
        st_copy(d, s, c).wait_recv()
        f = take(d, s + 1)

        @pl.loop(0, per)
        def _(i):
            hh = c * per + i
            theirs = got[d, s, hh]
            e = edge[d, hh, dim : dim + 1, :]
            edge[d, hh, 0:dim, :] = edge[d, hh, 0:dim, :] + (f * jnp.exp(e)) * theirs[0:dim]
            edge[d, hh, dim:, :] = edge[d, hh, dim:, :] + f * theirs[dim:]
            if s + 1 < chips:
                total, span = joined(f, sent[d, s, hh], theirs)
                sent[d, s + 1, hh, 0:dim, :] = total
                sent[d, s + 1, hh, dim:, :] = span

        if s + 1 < chips:
            st_copy(d, s + 1, c).start()
        else:
            fin_copy(d, c).start()

    def step_last(d):
        f = take(d, 0)

        def put(h, e):
            span = other[d, h, dim : dim + 1, :]
            state[d, h] = (jnp.exp(span * f) * e + f * other[d, h, 0:dim, :]).astype(BF16)

        @pl.loop(0, half)
        def _(hh):
            put(core * half + hh, edge[d, hh, 0:dim, :])

        for c in range(CHUNKS):
            fin_copy(d, c).wait_recv()

            @pl.loop(0, per)
            def _(i):
                hh = c * per + i
                put((1 - core) * half + hh, far[d, hh, 0:dim, :])

    order = sorted(((s, c) for s in range(chips) for c in range(CHUNKS)), key=lambda p: (2 * p[0] + p[1], p[0]))

    def exchange_beside(d, body):
        trips = heads // 2
        s0_copy(d).start()
        early = min(2, trips)
        inside = order[: max(0, (trips - early) // 2)]

        @pl.loop(0, trips)
        def _(i):
            body(2 * i)
            body(2 * i + 1)

            @pl.when(i == early - 1)
            def _():
                step_first(d)

            for n, (s, c) in enumerate(inside):

                @pl.when(i == early + 2 * n + 1)
                def _():
                    step(d, s, c)

        for s, c in order[len(inside) :]:
            step(d, s, c)
        step_last(d)

    tiles = [(i, j) for i in range(nb) for j in range(i + 1)]
    keep = (
        lax.broadcasted_iota(jnp.int32, (block, block), 0)
        >= lax.broadcasted_iota(jnp.int32, (block, block), 1)
    )

    def decay_of(h, i, j):
        col = cols[h, i * block : (i + 1) * block, :]
        col = jnp.concatenate([col] * (block // dim), axis=1)
        row = rows[pl.ds(h, 1), j * block : (j + 1) * block]
        value = jnp.exp(jnp.minimum(col - row, 0.0))
        return jnp.where(keep, value, 0.0) if i == j else value

    def span_of(i):
        return slice(i * block, (i + 1) * block)

    def intra(h):
        for i in range(nb):
            total = None
            for j in range(i + 1):
                s = nt(q[span_of(i), lane(h)], k[span_of(j), lane(h)])
                p = (s * decay_of(h, i, j)).astype(BF16)
                probs[h, tiles.index((i, j))] = p
                o = nn(p, v[span_of(j), lane(h)])
                total = o if total is None else total + o
            attn[span_of(i), lane(h)] = total

    loads[3].wait()
    pl.semaphore_wait(barrier, bits + n_tp - 1)
    exchange_beside(0, intra)

    loads[4].wait()
    loads[5].wait()
    scale_ref[...] = jnp.zeros_like(scale_ref)
    center_ref[...] = jnp.zeros_like(center_ref)

    def finish_attn(h):
        for i in range(nb):
            r = span_of(i)
            a = attn[r, lane(h)] + jnp.exp(cols[h, r, :]) * nn(q[r, lane(h)], state[0, h])
            attn[r, lane(h)] = a
            scale_ref[r, :] = scale_ref[r, :] + a * a
            sig = jax.nn.sigmoid(gate[r, lane(h)].astype(F32))
            center_ref[r, :] = center_ref[r, :] + up[r, lane(h)].astype(F32) * sig * a

    pairs(finish_attn)

    ones = jnp.ones((8, dim), F32)

    def lanes_summed(x):
        return lax.dot_general(
            ones, x, (((1,), (1,)), ((), ())), precision=HIGH, preferred_element_type=F32
        )

    sums[0:8, :] = lanes_summed(scale_ref[...])
    sums[8:16, :] = lanes_summed(center_ref[...])

    def tp_copy(d):
        return pltpu.make_async_remote_copy(
            src_ref=sums, dst_ref=sums_in.at[d - 1], send_sem=tp_send.at[d - 1],
            recv_sem=tp_recv.at[d - 1], device_id=(me, lax.rem(z + d, n_tp)), device_id_type=MESH,
        )

    for d in range(1, n_tp):
        tp_copy(d).start()
    total = sums[...]
    for d in range(1, n_tp):
        tp_copy(d).wait_recv()
        total = total + sums_in[d - 1]

    def spread(x):
        return lax.dot_general(
            x, ones / 8.0, (((0,), (0,)), ((), ())), precision=HIGH, preferred_element_type=F32
        )

    scale = lax.rsqrt(spread(total[0:8]) / width + 1e-06)
    scale_ref[...] = scale
    center_ref[...] = spread(total[8:16]) * scale / width

    def pointwise(h):
        weighted = None
        for i in range(nb):
            r = span_of(i)
            sc = scale_ref[r, :]
            normed = attn[r, lane(h)] * sc
            sig = jax.nn.sigmoid(gate[r, lane(h)].astype(F32))
            dnorm = up[r, lane(h)].astype(F32) * sig
            g = (sc * (dnorm - normed * center_ref[r, :])).astype(BF16)
            grad[r, lane(h)] = g
            up[r, lane(h)] = (normed * sig).astype(BF16)
            gate[r, lane(h)] = (dnorm * normed * (1.0 - sig)).astype(BF16)
            grown = (q[r, lane(h)].astype(F32) * jnp.exp(cols[h, r, :])).astype(BF16)
            w = tn(grown, g)
            weighted = w if weighted is None else weighted + w
        own[1, h, 0:dim, :] = weighted
        own[1, h, dim : dim + EXTRA, :] = own[0, h, dim : dim + EXTRA, :]

    pairs(pointwise)

    outs = [
        pltpu.make_async_copy(a, b, out_sem.at[i])
        for i, (a, b) in enumerate(
            ((up, out_hbm), (gate, gg_hbm), (q, dq_hbm), (k, dk_hbm), (v, dv_hbm))
        )
    ]
    outs[0].start()
    outs[1].start()

    def backward(h):
        dq = [None] * nb
        dk = [None] * nb
        dv = [None] * nb

        def add(parts, n, x):
            parts[n] = x if parts[n] is None else parts[n] + x

        for i, j in tiles:
            g = grad[span_of(i), lane(h)]
            pg = (nt(g, v[span_of(j), lane(h)]) * decay_of(h, i, j)).astype(BF16)
            add(dq, i, nn(pg, k[span_of(j), lane(h)]))
            add(dk, j, tn(pg, q[span_of(i), lane(h)]))
            add(dv, j, tn(probs[h, tiles.index((i, j))], g))
        for i in range(nb):
            r = span_of(i)
            carried = jnp.exp(cols[h, r, :]) * nt(grad[r, lane(h)], state[0, h])
            q[r, lane(h)] = (dq[i] + carried).astype(BF16)
            attn[r, lane(h)] = dk[i]
            dvp[r, lane(h)] = dv[i]

    exchange_beside(1, backward)
    outs[2].start()

    def finish(h):
        last = cols[h, tokens - 1 : tokens, :]
        for i in range(nb):
            r = span_of(i)
            tail = jnp.exp(last - cols[h, r, :])
            kk, vv = k[r, lane(h)], v[r, lane(h)]
            dk = attn[r, lane(h)] + tail * nt(vv, state[1, h])
            dv = dvp[r, lane(h)] + tail * nn(kk, state[1, h])
            k[r, lane(h)] = dk.astype(BF16)
            v[r, lane(h)] = dv.astype(BF16)

    pairs(finish)
    outs[3].start()
    outs[4].start()

    for d in (0, 1):
        s0_copy(d).wait_send()
        for c in range(CHUNKS):
            for s in range(chips):
                st_copy(d, s, c).wait_send()
            fin_copy(d, c).wait_send()
    for d in range(1, n_tp):
        tp_copy(d).wait_send()
    for c in outs:
        c.wait()


def solution(mesh):
    n_seq, n_tp = mesh.shape["seq"], mesh.shape["tp"]

    def shards(queries, keys, values, gate, log_decay, out_grad):
        tokens, flat = queries.shape
        heads = log_decay.shape[1]
        dim = flat // heads
        half = heads // 2
        chips = n_seq.bit_length() - 2
        block = min(256, tokens)
        nb = tokens // block
        big = pltpu.VMEM((tokens, flat), BF16)
        wide = pltpu.VMEM((tokens, flat), F32)
        message = (dim + EXTRA, dim)
        dma = pltpu.SemaphoreType.DMA
        any_spec = pl.BlockSpec(memory_space=pl.ANY)
        flops = 2 * tokens * tokens * flat * 5 + 2 * tokens * flat * dim * 7
        return tuple(
            pl.pallas_call(
                functools.partial(kernel, n_seq, n_tp, heads, dim, tokens),
                out_shape=[jax.ShapeDtypeStruct((tokens, flat), BF16)] * 5,
                in_specs=[any_spec] * 6,
                out_specs=[any_spec] * 5,
                scratch_shapes=[
                    big, big, big, big, pltpu.VMEM((tokens, heads), F32), big,
                    pltpu.VMEM((tokens, 128), F32), pltpu.VMEM((128, tokens), F32),
                    pltpu.VMEM((heads, tokens, dim), F32), wide, wide, big,
                    pltpu.VMEM((heads, nb * (nb + 1) // 2, block, block), BF16),
                    pltpu.VMEM((2, heads, *message), F32),
                    pltpu.VMEM((2, heads, *message), F32),
                    pltpu.VMEM((2, max(chips, 1), half, *message), F32),
                    pltpu.VMEM((2, max(chips, 1), half, *message), F32),
                    pltpu.VMEM((2, half, *message), F32),
                    pltpu.VMEM((2, half, *message), F32),
                    pltpu.VMEM((2, heads, dim, dim), BF16),
                    pltpu.VMEM((16, tokens), F32),
                    pltpu.VMEM((max(n_tp - 1, 1), 16, tokens), F32),
                    pltpu.VMEM((tokens, dim), F32), pltpu.VMEM((tokens, dim), F32),
                    dma((6,)), dma((5,)), dma((2,)), dma((2,)),
                    dma((2, max(chips, 1), CHUNKS)), dma((2, max(chips, 1), CHUNKS)),
                    dma((2, CHUNKS)), dma((2, CHUNKS)),
                    dma((max(n_tp - 1, 1),)), dma((max(n_tp - 1, 1),)),
                ],
                compiler_params=pltpu.CompilerParams(
                    collective_id=0, has_side_effects=True, vmem_limit_bytes=58 << 20
                ),
                cost_estimate=pl.CostEstimate(
                    flops=flops, bytes_accessed=tokens * flat * 20, transcendentals=0
                ),
            )(queries, keys, values, gate, log_decay, out_grad)
        )

    spec = P("seq", "tp")
    return jax.shard_map(
        shards, mesh=mesh, in_specs=(spec,) * 6, out_specs=(spec,) * 5, check_vma=False
    )
```

time: 229 us -> 90.3 us (0.39); the launches traced: 225 us -> 90 us
  matrix products: 78.5 us -> 0 us
  Pallas kernels: 0 us -> 76.1 us
  waiting for transfers between devices: 51.3 us -> 0 us
  blocking collectives: 26.6 us -> 0 us
  local copies, waits for them, and re-layouts: 36.3 us -> 13.3 us
  other arithmetic: 17.8 us -> 0 us
  between operations: 14.6 us -> 0.65 us
    dot_general x13 -> x0, matrix products: 78.5 us -> none  [the longest x1 15.7 us: shards(): state = jnp.einsum('mh,mhde->hde', weights, piece, precision=HIGH)]
    pallas_call x0 -> x1, Pallas kernels: none -> 76.1 us  [shards(): pl.pallas_call(functools.partial(kernel, n_seq, n_tp, heads, dim, tokens)...]
    all_gather x2 -> x0, waiting for transfers between devices: 51.2 us -> none  [the longest x1 27 us: shards(): piece = lax.all_gather(local[None], 'seq', axis=0, tiled=True)]
    psum x2 -> x0, blocking collectives: 16.3 us -> none  [the longest x1 9.63 us: shards(): squares = lax.psum(jnp.sum(attn * attn, axis=1), 'tp')]
    unnamed x27 -> x14, local copies, waits for them, and re-layouts: 25.7 us -> 13.3 us
    all_gather x1 -> x0, blocking collectives: 10.3 us -> none  [shards(): rates_all = lax.all_gather(last[None, :], 'seq', axis=0, tiled=True)]
    reshape x3 -> x0, local copies, waits for them, and re-layouts: 10.2 us -> none  [the longest x1 5.37 us: shards(): attn = (intra + inter).reshape(tokens, heads * HEAD)]
    convert_element_type x1 -> x0, other arithmetic: 7.11 us -> none  [shards(): gate_grad = (upstream * normed * sig * (1.0 - sig)).astype(jnp.bfloat16)]
  transfers between devices with their start and end apart: 2 -> 0, of which waited for: 2 -> 0; matrix products, arithmetic and copies ran while one was open for 21% -> 0% of each run, Pallas kernels for 0% -> 0%
where the time goes in v1:
time: 90.3 us; the launch traced here: 90 us
  Pallas kernels  76.1 us (84%)
  local copies, waits for them, and re-layouts  13.3 us (15%)
    pallas_call x1, Pallas kernels, shards(): pl.pallas_call(functools.partial(kernel, n_seq, n_tp, heads, dim, tokens)...  76.1 us
    unnamed x14, local copies, waits for them, and re-layouts  13.3 us

profile of v1, /device:TPU:1, one launch (start us, length us, event | category | flops | bytes accessed | tf_op | source)
XLA Modules:
  0.0 90.0 jit_solution(10768055731945722184)
XLA Ops:
  0.6 1.6 %copy.11.rate_hbm = f32[512,16]{1,0:T(8,128)} copy(f32[512,16]{0,1:T(8,128)} %param.10) | data formatting | bytes 65536 | tf_op args[4]
  2.2 76.1 %shard_map.101 = (bf16[512,2048]{1,0:T(8,128)(2,1)}, bf16[512,2048]{1,0:T(8,128)(2,1)}, bf16[512,2048]{1,0:T(8,128)(2,1)}, bf16[512,2048]{1,0:T(8,128)(2,1)}, bf16[512,2048]{1,0:T(8,128)(2,1)}) custom-call(bf16[512,2048]{1,0:T(8,128)(2,1)} %q_hbm.1, bf16[512,2048]{1,0:T(8,128)(2,1)} %k_hbm.1, bf16[512,2048]{1,0:T(8,128)(2,1)} %v_hbm.1, ...), custom_call_target="tpu_custom_call" | custom-call | flops 7247757312 | bytes 20971520 | tf_op jit(solution)/shard_map/pallas_call | solution.py:397
  78.3 0.0 copy-start.3
  78.3 3.3 %copy.17 = bf16[512,2048]{1,0:T(8,128)(2,1)} copy(bf16[512,2048]{1,0:T(8,128)(2,1)} %get-tuple-element.10) | data formatting | bytes 4194304
  81.6 0.0 copy-done.3
  81.6 0.0 copy-start.2
  81.6 1.3 %copy.18 = bf16[512,2048]{1,0:T(8,128)(2,1)} copy(bf16[512,2048]{1,0:T(8,128)(2,1)S(1)} %copy-done.3) | data formatting | bytes 4194304
  83.0 1.0 %copy-done.2 = bf16[512,2048]{1,0:T(8,128)(2,1)S(1)} copy-done((bf16[512,2048]{1,0:T(8,128)(2,1)S(1)}, bf16[512,2048]{1,0:T(8,128)(2,1)}, u32[]{:S(2)}) %copy-start.2) | copy-done | bytes 2097176
  84.0 0.0 copy-start.1
  84.0 1.3 %copy.19 = bf16[512,2048]{1,0:T(8,128)(2,1)} copy(bf16[512,2048]{1,0:T(8,128)(2,1)S(1)} %copy-done.2) | data formatting | bytes 4194304
  85.3 1.0 %copy-done.1 = bf16[512,2048]{1,0:T(8,128)(2,1)S(1)} copy-done((bf16[512,2048]{1,0:T(8,128)(2,1)S(1)}, bf16[512,2048]{1,0:T(8,128)(2,1)}, u32[]{:S(2)}) %copy-start.1) | copy-done | bytes 2097176
  86.3 0.0 copy-start
  86.3 1.3 %copy.20 = bf16[512,2048]{1,0:T(8,128)(2,1)} copy(bf16[512,2048]{1,0:T(8,128)(2,1)S(1)} %copy-done.1) | data formatting | bytes 4194304
  87.7 1.0 %copy-done = bf16[512,2048]{1,0:T(8,128)(2,1)S(1)} copy-done((bf16[512,2048]{1,0:T(8,128)(2,1)S(1)}, bf16[512,2048]{1,0:T(8,128)(2,1)}, u32[]{:S(2)}) %copy-start) | copy-done | bytes 2097176
  88.7 1.3 %copy.21 = bf16[512,2048]{1,0:T(8,128)(2,1)} copy(bf16[512,2048]{1,0:T(8,128)(2,1)S(1)} %copy-done) | data formatting | bytes 4194304
Async XLA Ops:
  78.3 3.3 %copy-start.3 = (bf16[512,2048]{1,0:T(8,128)(2,1)S(1)}, bf16[512,2048]{1,0:T(8,128)(2,1)}, u32[]{:S(2)}) copy-start(bf16[512,2048]{1,0:T(8,128)(2,1)} %get-tuple-element.11) | copy-start | bytes 6291460
  81.6 2.3 %copy-start.2 = (bf16[512,2048]{1,0:T(8,128)(2,1)S(1)}, bf16[512,2048]{1,0:T(8,128)(2,1)}, u32[]{:S(2)}) copy-start(bf16[512,2048]{1,0:T(8,128)(2,1)} %get-tuple-element.12) | copy-start | bytes 6291460
  84.0 2.3 %copy-start.1 = (bf16[512,2048]{1,0:T(8,128)(2,1)S(1)}, bf16[512,2048]{1,0:T(8,128)(2,1)}, u32[]{:S(2)}) copy-start(bf16[512,2048]{1,0:T(8,128)(2,1)} %get-tuple-element.13) | copy-start | bytes 6291460
  86.3 2.3 %copy-start = (bf16[512,2048]{1,0:T(8,128)(2,1)S(1)}, bf16[512,2048]{1,0:T(8,128)(2,1)}, u32[]{:S(2)}) copy-start(bf16[512,2048]{1,0:T(8,128)(2,1)} %get-tuple-element.14) | copy-start | bytes 6291460

commit v2 on v1

--- a/solution.py
+++ b/solution.py
@@ -83,15 +83,16 @@
 
     loads[0].wait()
     rates_wide[...] = jnp.zeros_like(rates_wide)
-    rates_wide[:, 0:heads] = rate[...]
+    rates_wide[0:heads, :] = rate[...]
     tri = (
         lax.broadcasted_iota(jnp.int32, (tokens, tokens), 0)
         >= lax.broadcasted_iota(jnp.int32, (tokens, tokens), 1)
     ).astype(F32)
-    within = lax.dot_general(
-        tri, rates_wide[...], (((1,), (0,)), ((), ())), precision=HIGH, preferred_element_type=F32
+    across = lax.dot_general(
+        rates_wide[...], tri, (((1,), (1,)), ((), ())), precision=HIGH, preferred_element_type=F32
     )
-    rows[...] = within.T
+    rows[...] = across
+    within = across.T
     for h in range(heads):
         cols[h] = jnp.broadcast_to(within[:, h : h + 1], (tokens, dim))
 
@@ -376,6 +377,11 @@
         c.wait()
 
 
+def hand_on(*refs):
+    for source, target in zip(refs[:5], refs[5:]):
+        target[...] = source[...]
+
+
 def solution(mesh):
     n_seq, n_tp = mesh.shape["seq"], mesh.shape["tp"]
 
@@ -393,15 +399,15 @@
         dma = pltpu.SemaphoreType.DMA
         any_spec = pl.BlockSpec(memory_space=pl.ANY)
         flops = 2 * tokens * tokens * flat * 5 + 2 * tokens * flat * dim * 7
-        return tuple(
+        results = tuple(
             pl.pallas_call(
                 functools.partial(kernel, n_seq, n_tp, heads, dim, tokens),
                 out_shape=[jax.ShapeDtypeStruct((tokens, flat), BF16)] * 5,
                 in_specs=[any_spec] * 6,
                 out_specs=[any_spec] * 5,
                 scratch_shapes=[
-                    big, big, big, big, pltpu.VMEM((tokens, heads), F32), big,
-                    pltpu.VMEM((tokens, 128), F32), pltpu.VMEM((128, tokens), F32),
+                    big, big, big, big, pltpu.VMEM((heads, tokens), F32), big,
+                    pltpu.VMEM((128, tokens), F32), pltpu.VMEM((128, tokens), F32),
                     pltpu.VMEM((heads, tokens, dim), F32), wide, wide, big,
                     pltpu.VMEM((heads, nb * (nb + 1) // 2, block, block), BF16),
                     pltpu.VMEM((2, heads, *message), F32),
@@ -425,7 +431,17 @@
                 cost_estimate=pl.CostEstimate(
                     flops=flops, bytes_accessed=tokens * flat * 20, transcendentals=0
                 ),
-            )(queries, keys, values, gate, log_decay, out_grad)
+            )(queries, keys, values, gate, log_decay.T, out_grad)
+        )
+        strip = pl.BlockSpec((tokens, flat // 4), lambda i: (0, i))
+        return tuple(
+            pl.pallas_call(
+                hand_on,
+                grid=(4,),
+                out_shape=[jax.ShapeDtypeStruct((tokens, flat), BF16)] * 5,
+                in_specs=[strip] * 5,
+                out_specs=[strip] * 5,
+            )(*results)
         )
 
     spec = P("seq", "tp")

time: 90.3 us -> 84.6 us (0.937)
  local copies, waits for them, and re-layouts: 13.3 us -> 0 us
  Pallas kernels: 76.1 us -> 83.8 us
    unnamed x14 -> x0, local copies, waits for them, and re-layouts: 13.3 us -> none
    pallas_call x0 -> x1, Pallas kernels: none -> 8.13 us  [shards(): pl.pallas_call(hand_on, grid=(4,), out_shape=[jax.ShapeDtypeStruct((token...]
where the time goes in v2:
time: 84.6 us; the launch traced here: 84.5 us
  Pallas kernels  83.8 us (99%)
    pallas_call x1, Pallas kernels, shards(): pl.pallas_call(functools.partial(kernel, n_seq, n_tp, heads, dim, tokens)...  75.7 us
    pallas_call x1, Pallas kernels, shards(): pl.pallas_call(hand_on, grid=(4,), out_shape=[jax.ShapeDtypeStruct((token...  8.13 us

profile of v2, /device:TPU:1, one launch (start us, length us, event | category | flops | bytes accessed | tf_op | source)
XLA Modules:
  0.0 84.5 jit_solution(3514637984565778496)
XLA Ops:
  0.6 75.7 %shard_map.101 = (bf16[512,2048]{1,0:T(8,128)(2,1)}, bf16[512,2048]{1,0:T(8,128)(2,1)}, bf16[512,2048]{1,0:T(8,128)(2,1)}, bf16[512,2048]{1,0:T(8,128)(2,1)}, bf16[512,2048]{1,0:T(8,128)(2,1)}) custom-call(bf16[512,2048]{1,0:T(8,128)(2,1)} %q_hbm.1, bf16[512,2048]{1,0:T(8,128)(2,1)} %k_hbm.1, bf16[512,2048]{1,0:T(8,128)(2,1)} %v_hbm.1, ...), custom_call_target="tpu_custom_call" | custom-call | flops 7247757312 | bytes 20971520 | tf_op jit(solution)/shard_map/pallas_call | solution.py:403
  76.4 8.1 %shard_map.102 = (bf16[512,2048]{1,0:T(8,128)(2,1)}, bf16[512,2048]{1,0:T(8,128)(2,1)}, bf16[512,2048]{1,0:T(8,128)(2,1)}, bf16[512,2048]{1,0:T(8,128)(2,1)}, bf16[512,2048]{1,0:T(8,128)(2,1)}) custom-call(bf16[512,2048]{1,0:T(8,128)(2,1)} %get-tuple-element.10.refs_0_, bf16[512,2048]{1,0:T(8,128)(2,1)} %get-tuple-element.11.refs_1_, ...), custom_call_target="tpu_custom_call" | custom-call | tf_op jit(solution)/shard_map/pallas_call | solution.py:438
